TPU v7x, 256 devices: a whole 4x4x8 slice. The times are simulated.
256 devices in a mesh: rows: 64 (over z, y, core), mem: 4 (over x).
Axes of the slice: x: 4, y: 4, z: 8, core: 2. Of those that a mesh axis runs over, the one named last changes fastest.
Arguments:
- control: bfloat16 [16, 32, 2, 512, 512], P('mem', None, None, 'rows'), may hold values from -6 to 6
- vert_root: float32 [32, 32], replicated, may hold values from -1 to 1
- loc_spec: float32 [512], replicated, may hold values from 0.1 to 1
- legendre: bfloat16 [512, 512, 768], P('rows'), as said below
- wave_table: int32 [512], replicated, may hold values from 0 to 511, as said below
- lat_order: int32 [768], replicated, may hold values from 0 to 767, each once
- perturb: bfloat16 [768, 16, 32, 1536], P('rows', None, 'mem'), may hold values from -3 to 3
Outputs:
- increment: bfloat16 [768, 32, 1536], P('rows', 'mem')
Inputs may be any that keep to these rules, and one draw needn't show every extreme that they name: `wave_table`: every zonal wavenumber 0 to 511 sits in exactly one slot; the slots held by one index of rows are pairs m and 511 - m. legendre[s, n, t] is zero where n < wave_table[s]. `lat_order`: a permutation.
All inputs are finite; a program needn't handle non-finite values.
Results may differ from a plain program's by a relative error of at most 0.0085.
Values may be sent and summed in bfloat16 or wider, within the bound.
A program may use at most 128 MiB of HBM per device.

v0:
```python
import functools
import math

import jax
import jax.numpy as jnp
from jax import lax
from jax.experimental import pallas as pl
from jax.experimental.pallas import tpu as pltpu
from jax.sharding import PartitionSpec as P

HALVES = 2
LATS = 4
VMEM_LIMIT = 56 * 1024 * 1024


def make_basis(wave_table, lon_count):
    longitude = lax.iota(jnp.int32, lon_count)
    phases = wave_table[:, None] * longitude[None, :] % lon_count
    angles = phases.astype(jnp.float32) * (2.0 * math.pi / lon_count)
    weights = jnp.where(wave_table == 0, 1.0, 2.0).astype(jnp.float32)[:, None]
    return jnp.stack([weights * jnp.cos(angles), -weights * jnp.sin(angles)]).astype(jnp.bfloat16)


def legendre_kernel(*refs):
    specs, (leg_ref, order_ref, out_ref) = refs[:-3], refs[-3:]
    members, parts, _, levels, totals = specs[0].shape
    rows = [
        s[:, r, 0].reshape(members * levels, totals) for r in range(parts) for s in specs
    ]
    spec = jnp.concatenate(rows, axis=0)
    fourier = jnp.dot(spec, leg_ref[0], preferred_element_type=jnp.float32).astype(jnp.bfloat16)
    stored = lax.dot_general(
        order_ref[...], fourier, (((1,), (1,)), ((), ())), preferred_element_type=jnp.float32
    ).astype(jnp.bfloat16)
    lats = out_ref.shape[2]
    for d in range(out_ref.shape[0]):
        out_ref[d, 0] = stored[d * lats : (d + 1) * lats]


def legendre_step(specs, legendre, order, first, row_count):
    members, parts, slots, levels, totals = specs[0].shape
    lat_count = legendre.shape[2]
    lats = lat_count // row_count
    width = len(specs) * members * parts * levels
    flops = 2 * slots * width * lat_count * (totals + lat_count)
    return pl.pallas_call(
        legendre_kernel,
        grid=(slots,),
        out_shape=jax.ShapeDtypeStruct((row_count, slots, lats, width), jnp.bfloat16),
        in_specs=[
            pl.BlockSpec((members, parts, 1, levels, totals), lambda s: (0, 0, s, 0, 0))
            for _ in specs
        ]
        + [
            pl.BlockSpec((1, totals, lat_count), lambda s: (first + s, 0, 0)),
            pl.BlockSpec((lat_count, lat_count), lambda s: (0, 0)),
        ],
        out_specs=pl.BlockSpec((row_count, 1, lats, width), lambda s: (0, s, 0, 0)),
        compiler_params=pltpu.CompilerParams(vmem_limit_bytes=VMEM_LIMIT),
        cost_estimate=pl.CostEstimate(
            flops=flops,
            bytes_accessed=2 * slots * (totals + width) * lat_count,
            transcendentals=0,
        ),
    )(*specs, legendre, order)


def zonal_kernel(chunks, half, *refs):
    fours, (basis_ref, ptb_ref, before_ref, out_ref) = refs[:chunks], refs[chunks:]
    lats, members, levels, lon_count = ptb_ref.shape
    mem_count = lax.axis_size("mem")
    me = lax.axis_index("mem")
    share = members // mem_count
    taken = share // HALVES
    width = fours[0].shape[2] // 2
    blocks = []
    for j in range(lats):
        pairs = [f[j].T for f in fours]
        blocks.append(
            jnp.concatenate([p[r * width : (r + 1) * width] for p in pairs for r in range(2)], axis=1)
        )
    lhs = jnp.concatenate(blocks, axis=0)
    piece = 512 if lon_count % 512 == 0 else lon_count
    for x in range(0, lon_count, piece):
        field = jnp.dot(lhs, basis_ref[:, x : x + piece], preferred_element_type=jnp.float32)
        field = field.astype(jnp.bfloat16).astype(jnp.float32)
        field = field.reshape(lats, mem_count, taken, levels, piece)
        total = jnp.zeros((lats, levels, piece), jnp.float32)
        if half > 0:
            total = before_ref[:, :, x : x + piece]
        for i in range(mem_count):
            source = lax.rem(me + mem_count - i, mem_count)
            begin = source * share + half * taken
            ptb = ptb_ref[:, pl.ds(begin, taken), :, x : x + piece].astype(jnp.float32)
            total += jnp.sum(field[:, i] * ptb, axis=1)
        out_ref[:, :, x : x + piece] = total.astype(out_ref.dtype)


def zonal_step(fours, basis, perturb, half, before):
    lats, members, levels, lon_count = perturb.shape
    width = fours[0].shape[2]
    depth = basis.shape[0]
    block = math.gcd(LATS, lats)
    out_type = jnp.bfloat16 if half == HALVES - 1 else jnp.float32
    row = pl.BlockSpec((block, levels, lon_count), lambda j: (j, 0, 0))
    kept = row if half > 0 else pl.BlockSpec((1, 8, 128), lambda j: (0, 0, 0))
    return pl.pallas_call(
        functools.partial(zonal_kernel, len(fours), half),
        grid=(lats // block,),
        out_shape=jax.ShapeDtypeStruct((lats, levels, lon_count), out_type),
        in_specs=[
            pl.BlockSpec((block, f.shape[1], width), lambda j: (j, 0, 0)) for f in fours
        ]
        + [
            pl.BlockSpec((depth, lon_count), lambda j: (0, 0)),
            pl.BlockSpec((block, members, levels, lon_count), lambda j: (j, 0, 0, 0)),
            kept,
        ],
        out_specs=row,
        compiler_params=pltpu.CompilerParams(vmem_limit_bytes=VMEM_LIMIT),
        cost_estimate=pl.CostEstimate(
            flops=lats * depth * width * lon_count,
            bytes_accessed=2 * perturb.size,
            transcendentals=0,
        ),
    )(*fours, basis, perturb, before)


def ordered_basis(wave_table, parts, row_count, lon_count):
    table = wave_table.reshape(row_count, -1)
    pieces, first = [], 0
    basis = make_basis(table.reshape(-1), lon_count).reshape(2, row_count, -1, lon_count)
    for slots in parts:
        pieces.append(basis[:, :, first : first + slots].reshape(-1, lon_count))
        first += slots
    return jnp.concatenate(pieces, axis=0)


def shards(control, vert_root, loc_spec, legendre, wave_table, lat_order, perturb):
    mem_count = lax.axis_size("mem")
    row_count = lax.axis_size("rows")
    members, levels, _, slot_count, totals = control.shape
    lat_count = legendre.shape[2]
    share = levels // mem_count
    me = lax.axis_index("mem")
    root = vert_root.reshape(mem_count, share, levels).astype(jnp.bfloat16)
    root = jnp.take(root, (me + lax.iota(jnp.int32, mem_count)) % mem_count, axis=0)
    order = (lat_order[:, None] == lax.iota(jnp.int32, lat_count)[None, :]).astype(jnp.bfloat16)

    taken = members // HALVES
    eighth = slot_count // 8
    splits = [(2 * eighth, 3 * eighth, 3 * eighth), (4 * eighth, 4 * eighth)]
    partial = jnp.zeros((1, 8, 128), jnp.float32)
    for half, split in enumerate(splits):
        fours, first = [], 0
        for slots in split:
            spec = jnp.einsum(
                "dlv,kvrsn->dkrsln",
                root,
                control[half * taken : (half + 1) * taken, :, :, first : first + slots],
                preferred_element_type=jnp.float32,
            )
            spec = (spec * loc_spec).astype(jnp.bfloat16)
            specs = [spec[0]] + [
                lax.ppermute(spec[i], "mem", [(d, (d + i) % mem_count) for d in range(mem_count)])
                for i in range(1, mem_count)
            ]
            four = legendre_step(specs, legendre, order, first, row_count)
            four = lax.all_to_all(four, "rows", split_axis=0, concat_axis=0, tiled=True)
            four = four.reshape(row_count * slots, four.shape[2], four.shape[3]).swapaxes(0, 1)
            fours.append(four)
            first += slots
        basis = ordered_basis(wave_table, split, row_count, perturb.shape[3])
        partial = zonal_step(fours, basis, perturb, half, partial)
    return partial


def solution(mesh):
    return jax.shard_map(
        shards,
        mesh=mesh,
        in_specs=(
            P("mem", None, None, "rows", None),
            P(),
            P(),
            P("rows", None, None),
            P(),
            P(),
            P("rows", None, "mem", None),
        ),
        out_specs=P("rows", "mem", None),
        check_vma=False,
    )
```

profile of v0, /device:TPU:1, one launch (start us, length us, event | category | flops | bytes accessed | tf_op | source)
XLA Modules:
  0.0 212.5 jit_solution(7597643383217680175)
XLA Ops:
  0.8 1.4 slice.102
  4.3 2.0 collective-permute-start.6
  6.4 2.5 %collective-permute-start.7 = (bf16[2,2,2,8,512]{4,3,2,1,0:T(8,128)(2,1)S(1)}, bf16[2,2,2,8,512]{4,3,2,1,0:T(8,128)(2,1)S(1)}, u32[]{:S(2)}, u32[]{:S(2)}) collective-permute-start(bf16[2,2,2,8,512]{4,3,2,1,0:T(8,128)(2,1)S(1)} %get-tuple-element.30), channel_id=1, source_target_pairs={{0,2},{1,3},{2,0},{3,1},{4,6},{5,7},{6,4},{7,5},{8,10},{9,11},{10,... | collective-permute-start | bytes 196616 | tf_op jit(solution)/shard_map/ppermute | solution.py:165
  8.8 1.2 collective-permute-start.8
  10.0 2.0 fusion.5.refs_5_
  12.9 4.0 %shard_map.75 = bf16[64,2,12,128]{3,2,1,0:T(8,128)(2,1)} custom-call(bf16[2,2,2,8,512]{4,3,2,1,0:T(8,128)(2,1)} %get-tuple-element.32.refs_0_, bf16[2,2,2,8,512]{4,3,2,1,0:T(8,128)(2,1)} %copy-done.18, bf16[2,2,2,8,512]{4,3,2,1,0:T(8,128)(2,1)} %copy-done.19, bf16[2,2,2,8,512]{4,3,2,1,0:T(8,128)(2,1)} %copy-done.20, bf16[8,512,768]{2,1,0:T(8,128)(2,1)} %refs_4_.10, ...), custom_call_target="tpu_custom_call" | custom-call | flops 503316480 | bytes 1966080 | tf_op jit(solution)/shard_map/pallas_call | solution.py:46
  16.8 2.1 copy.35
  19.0 13.7 %all-to-all-start.2 = ((bf16[64,2,12,128]{3,1,2,0:T(2,128)(2,1)}), bf16[64,2,12,128]{3,1,2,0:T(2,128)(2,1)S(1)}, u32[]{:S(2)}, u32[]{:S(2)}) async-start(bf16[64,2,12,128]{3,1,2,0:T(2,128)(2,1)} %copy.35), calls=%async_computation.2 | async-start | bytes 786432 | tf_op jit(solution)/shard_map/all_to_all | solution.py:169
  34.5 3.3 %collective-permute-start.13 = (bf16[2,2,3,8,512]{4,3,2,1,0:T(8,128)(2,1)S(1)}, bf16[2,2,3,8,512]{4,3,2,1,0:T(8,128)(2,1)S(1)}, u32[]{:S(2)}, u32[]{:S(2)}) collective-permute-start(bf16[2,2,3,8,512]{4,3,2,1,0:T(8,128)(2,1)S(1)} %get-tuple-element.22), channel_id=1, source_target_pairs={{0,2},{1,3},{2,0},{3,1},{4,6},{5,7},{6,4},{7,5},{8,10},{9,11},{10,... | collective-permute-start | bytes 294920 | tf_op jit(solution)/shard_map/ppermute | solution.py:165
  37.8 1.6 collective-permute-done.12.refs_1_
  39.3 3.0 %collective-permute-done.13.refs_2_ = bf16[2,2,3,8,512]{4,3,2,1,0:T(8,128)(2,1)S(1)} collective-permute-done((bf16[2,2,3,8,512]{4,3,2,1,0:T(8,128)(2,1)S(1)}, bf16[2,2,3,8,512]{4,3,2,1,0:T(8,128)(2,1)S(1)}, u32[]{:S(2)}, u32[]{:S(2)}) %collective-permute-start.13) | collective-permute-done | bytes 98336 | tf_op jit(solution)/shard_map/ppermute | solution.py:165
  43.0 5.1 %shard_map.77 = bf16[64,3,12,128]{3,2,1,0:T(8,128)(2,1)} custom-call(bf16[2,2,3,8,512]{4,3,2,1,0:T(8,128)(2,1)} %get-tuple-element.24.refs_0_, bf16[2,2,3,8,512]{4,3,2,1,0:T(8,128)(2,1)} %copy-done.12, bf16[2,2,3,8,512]{4,3,2,1,0:T(8,128)(2,1)} %copy-done.14, bf16[2,2,3,8,512]{4,3,2,1,0:T(8,128)(2,1)} %copy-done.16, bf16[8,512,768]{2,1,0:T(8,128)(2,1)} %refs_4_.10, ...), custom_call_target="tpu_custom_call" | custom-call | flops 754974720 | bytes 2949120 | tf_op jit(solution)/shard_map/pallas_call | solution.py:46
  48.1 11.2 %all-to-all-start.4 = ((bf16[64,3,12,128]{3,2,1,0:T(8,128)(2,1)}), bf16[64,3,12,128]{3,2,1,0:T(8,128)(2,1)S(1)}, u32[]{:S(2)}, u32[]{:S(2)}) async-start(bf16[64,3,12,128]{3,2,1,0:T(8,128)(2,1)} %shard_map.77), calls=%async_computation.4 | async-start | bytes 1572864 | tf_op jit(solution)/shard_map/all_to_all | solution.py:169
  61.3 1.8 collective-permute-start.11
  63.1 2.7 %collective-permute-done.10.refs_2_ = bf16[2,2,3,8,512]{4,3,2,1,0:T(8,128)(2,1)S(1)} collective-permute-done((bf16[2,2,3,8,512]{4,3,2,1,0:T(8,128)(2,1)S(1)}, bf16[2,2,3,8,512]{4,3,2,1,0:T(8,128)(2,1)S(1)}, u32[]{:S(2)}, u32[]{:S(2)}) %collective-permute-start.10) | collective-permute-done | bytes 98336 | tf_op jit(solution)/shard_map/ppermute | solution.py:165
  65.7 1.8 collective-permute-done.11.refs_3_
  68.8 5.1 %shard_map.76 = bf16[64,3,12,128]{3,2,1,0:T(8,128)(2,1)} custom-call(bf16[2,2,3,8,512]{4,3,2,1,0:T(8,128)(2,1)} %get-tuple-element.28.refs_0_, bf16[2,2,3,8,512]{4,3,2,1,0:T(8,128)(2,1)} %copy-done.17, bf16[2,2,3,8,512]{4,3,2,1,0:T(8,128)(2,1)} %copy-done.13, bf16[2,2,3,8,512]{4,3,2,1,0:T(8,128)(2,1)} %copy-done.15, bf16[8,512,768]{2,1,0:T(8,128)(2,1)} %refs_4_.10, ...), custom_call_target="tpu_custom_call" | custom-call | flops 754974720 | bytes 2949120 | tf_op jit(solution)/shard_map/pallas_call | solution.py:46
  74.0 8.4 %all-to-all-done.4 = bf16[64,3,12,128]{3,2,1,0:T(8,128)(2,1)S(1)} async-done(((bf16[64,3,12,128]{3,2,1,0:T(8,128)(2,1)}), bf16[64,3,12,128]{3,2,1,0:T(8,128)(2,1)S(1)}, u32[]{:S(2)}, u32[]{:S(2)}) %all-to-all-start.4) | async-done | bytes 589856 | tf_op jit(solution)/shard_map/all_to_all | solution.py:169
  82.3 5.9 %all-to-all-start.3 = ((bf16[64,3,12,128]{3,2,1,0:T(8,128)(2,1)}), bf16[64,3,12,128]{3,2,1,0:T(8,128)(2,1)S(1)}, u32[]{:S(2)}, u32[]{:S(2)}) async-start(bf16[64,3,12,128]{3,2,1,0:T(8,128)(2,1)} %shard_map.76), calls=%async_computation.3 | async-start | bytes 1572864 | tf_op jit(solution)/shard_map/all_to_all | solution.py:169
  88.3 2.1 fusion.30
  91.7 2.9 %collective-permute-start.4 = (bf16[2,2,4,8,512]{4,3,2,1,0:T(8,128)(2,1)S(1)}, bf16[2,2,4,8,512]{4,3,2,1,0:T(8,128)(2,1)S(1)}, u32[]{:S(2)}, u32[]{:S(2)}) collective-permute-start(bf16[2,2,4,8,512]{4,3,2,1,0:T(8,128)(2,1)S(1)} %get-tuple-element.14), channel_id=1, source_target_pairs={{0,2},{1,3},{2,0},{3,1},{4,6},{5,7},{6,4},{7,5},{8,10},{9,11},{10,... | collective-permute-start | bytes 393224 | tf_op jit(solution)/shard_map/ppermute | solution.py:165
  95.0 2.2 %collective-permute-done.3.refs_1_ = bf16[2,2,4,8,512]{4,3,2,1,0:T(8,128)(2,1)S(1)} collective-permute-done((bf16[2,2,4,8,512]{4,3,2,1,0:T(8,128)(2,1)S(1)}, bf16[2,2,4,8,512]{4,3,2,1,0:T(8,128)(2,1)S(1)}, u32[]{:S(2)}, u32[]{:S(2)}) %collective-permute-start.3) | collective-permute-done | bytes 131104 | tf_op jit(solution)/shard_map/ppermute | solution.py:165
  97.2 3.4 %collective-permute-done.4.refs_2_ = bf16[2,2,4,8,512]{4,3,2,1,0:T(8,128)(2,1)S(1)} collective-permute-done((bf16[2,2,4,8,512]{4,3,2,1,0:T(8,128)(2,1)S(1)}, bf16[2,2,4,8,512]{4,3,2,1,0:T(8,128)(2,1)S(1)}, u32[]{:S(2)}, u32[]{:S(2)}) %collective-permute-start.4) | collective-permute-done | bytes 131104 | tf_op jit(solution)/shard_map/ppermute | solution.py:165
  101.3 5.9 %shard_map.74 = bf16[64,4,12,128]{3,2,1,0:T(8,128)(2,1)} custom-call(bf16[2,2,4,8,512]{4,3,2,1,0:T(8,128)(2,1)} %get-tuple-element.16.refs_0_, bf16[2,2,4,8,512]{4,3,2,1,0:T(8,128)(2,1)} %copy-done.9, bf16[2,2,4,8,512]{4,3,2,1,0:T(8,128)(2,1)} %copy-done.10, bf16[2,2,4,8,512]{4,3,2,1,0:T(8,128)(2,1)} %copy-done.11, bf16[8,512,768]{2,1,0:T(8,128)(2,1)} %refs_4_.10, ...), custom_call_target="tpu_custom_call" | custom-call | flops 1006632960 | bytes 3932160 | tf_op jit(solution)/shard_map/pallas_call | solution.py:46
  107.2 2.4 %copy.32 = bf16[64,4,12,128]{3,1,2,0:T(4,128)(2,1)} copy(bf16[64,4,12,128]{3,2,1,0:T(8,128)(2,1)} %shard_map.74) | data formatting | bytes 1572864 | tf_op jit(solution)/shard_map/pallas_call | solution.py:46
  109.6 1.6 all-to-all-done.3
  111.3 9.8 %all-to-all-start.1 = ((bf16[64,4,12,128]{3,1,2,0:T(4,128)(2,1)}), bf16[64,4,12,128]{3,1,2,0:T(4,128)(2,1)}, u32[]{:S(2)}, u32[]{:S(2)}) async-start(bf16[64,4,12,128]{3,1,2,0:T(4,128)(2,1)} %copy.32), calls=%async_computation.1 | async-start | bytes 1572864 | tf_op jit(solution)/shard_map/all_to_all | solution.py:169
  122.1 3.2 %collective-permute-start.1 = (bf16[2,2,4,8,512]{4,3,2,1,0:T(8,128)(2,1)}, bf16[2,2,4,8,512]{4,3,2,1,0:T(8,128)(2,1)}, u32[]{:S(2)}, u32[]{:S(2)}) collective-permute-start(bf16[2,2,4,8,512]{4,3,2,1,0:T(8,128)(2,1)} %get-tuple-element.18), channel_id=1, source_target_pairs={{0,2},{1,3},{2,0},{3,1},{4,6},{5,7},{6,4},{7,5},{8,10},{9,11},{10,... | collective-permute-start | bytes 393224 | tf_op jit(solution)/shard_map/ppermute | solution.py:165
  127.5 14.5 %multiply_convert_fusion = (bf16[1,64,8,1536]{3,2,1,0:T(8,128)(2,1)S(1)}, bf16[1,64,8,1536]{3,2,1,0:T(8,128)(2,1)S(1)}) fusion(f32[64,8]{1,0:T(8,128)} %mul.148, s32[64,8]{1,0:T(8,128)} %mul.142, f32[64,8]{1,0:T(8,128)} %mul.140), kind=kLoop, calls=%fused_computation.14 | loop fusion | flops 10223616 | bytes 3151872 | tf_op jit(solution)/shard_map/convert.1
  142.0 2.8 %fusion.6 = (bf16[2,64,3,1536]{3,2,1,0:T(4,128)(2,1)}, bf16[2,64,3,1536]{3,2,1,0:T(4,128)(2,1)}) fusion(bf16[1,64,8,1536]{3,2,1,0:T(8,128)(2,1)S(1)} %get-tuple-element.34, bf16[1,64,8,1536]{3,2,1,0:T(8,128)(2,1)S(1)} %get-tuple-element.33), kind=kLoop, calls=%fused_computation.22 | loop fusion | flops 4718592 | bytes 5505024 | tf_op jit(solution)/shard_map/stack | solution.py:21
  144.8 6.0 %shard_map.73 = bf16[64,4,12,128]{3,2,1,0:T(8,128)(2,1)} custom-call(bf16[2,2,4,8,512]{4,3,2,1,0:T(8,128)(2,1)} %get-tuple-element.20.refs_0_, bf16[2,2,4,8,512]{4,3,2,1,0:T(8,128)(2,1)} %collective-permute-done.refs_1_, bf16[2,2,4,8,512]{4,3,2,1,0:T(8,128)(2,1)} %collective-permute-done.1.refs_2_, ...), custom_call_target="tpu_custom_call" | custom-call | flops 1006632960 | bytes 3932160 | tf_op jit(solution)/shard_map/pallas_call | solution.py:46
  150.8 2.4 %copy.29 = bf16[64,4,12,128]{3,1,2,0:T(4,128)(2,1)} copy(bf16[64,4,12,128]{3,2,1,0:T(8,128)(2,1)} %shard_map.73) | data formatting | bytes 1572864 | tf_op jit(solution)/shard_map/pallas_call | solution.py:46
  153.3 11.0 %all-to-all-start = ((bf16[64,4,12,128]{3,1,2,0:T(4,128)(2,1)}), bf16[64,4,12,128]{3,1,2,0:T(4,128)(2,1)}, u32[]{:S(2)}, u32[]{:S(2)}) async-start(bf16[64,4,12,128]{3,1,2,0:T(4,128)(2,1)} %copy.29), calls=%async_computation | async-start | bytes 1572864 | tf_op jit(solution)/shard_map/all_to_all | solution.py:169
  164.3 1.4 fusion.19
  165.7 4.0 %reshape.203 = bf16[384,1536]{1,0:T(8,128)(2,1)} reshape(bf16[2,64,3,1536]{3,2,1,0:T(4,128)(2,1)} %get-tuple-element.5) | data formatting | bytes 2359296 | tf_op jit(solution)/shard_map/reshape | solution.py:134
  169.7 4.0 %reshape.204 = bf16[384,1536]{1,0:T(8,128)(2,1)} reshape(bf16[2,64,3,1536]{3,2,1,0:T(4,128)(2,1)} %get-tuple-element.6) | data formatting | bytes 2359296 | tf_op jit(solution)/shard_map/reshape | solution.py:134
  173.6 3.0 %reshape.202 = bf16[256,1536]{1,0:T(8,128)(2,1)} reshape(bf16[2,64,2,1536]{3,2,1,0:T(2,128)(2,1)} %fusion.19) | data formatting | bytes 1572864 | tf_op jit(solution)/shard_map/reshape | solution.py:134
  176.6 3.1 %fusion.7 = (bf16[2,64,4,1536]{3,2,1,0:T(4,128)(2,1)}, bf16[2,64,4,1536]{3,2,1,0:T(4,128)(2,1)}) fusion(bf16[1,64,8,1536]{3,2,1,0:T(8,128)(2,1)S(1)} %get-tuple-element.34, bf16[1,64,8,1536]{3,2,1,0:T(8,128)(2,1)S(1)} %get-tuple-element.33), kind=kLoop, calls=%fused_computation.23 | loop fusion | flops 1572864 | bytes 6291456 | tf_op jit(solution)/shard_map/stack | solution.py:21
  179.7 2.8 %reshape.197 = bf16[512,1536]{1,0:T(8,128)(2,1)S(1)} reshape(bf16[2,64,4,1536]{3,2,1,0:T(4,128)(2,1)} %get-tuple-element.7) | data formatting | bytes 3145728 | tf_op jit(solution)/shard_map/reshape | solution.py:134
  182.5 1.4 reshape.198
  183.9 3.4 %pad_maximum_fusion.refs_2_ = bf16[1024,1536]{1,0:T(8,128)(2,1)} fusion(bf16[512,1536]{1,0:T(8,128)(2,1)} %reshape.198, bf16[512,1536]{1,0:T(8,128)(2,1)S(1)} %reshape.197), kind=kLoop, calls=%fused_computation.12 | loop fusion | flops 6291456 | bytes 6291456 | tf_op jit(solution)/shard_map/concatenate | solution.py:136
  187.3 1.9 pad_maximum_fusion.1.refs_3_
  189.2 1.1 copy.36
  190.3 1.0 copy.61
  192.9 7.7 %shard_map.78.refs_4_ = f32[12,8,1536]{2,1,0:T(8,128)} custom-call(bf16[12,128,128]{2,1,0:T(8,128)(2,1)} %bitcast.105, bf16[12,192,128]{2,1,0:T(8,128)(2,1)} %bitcast.104, bf16[12,192,128]{2,1,0:T(8,128)(2,1)} %bitcast.103, bf16[1024,1536]{1,0:T(8,128)(2,1)} %pad_maximum_fusion.1.refs_3_, bf16[12,16,8,1536]{3,2,1,0:T(8,128)(2,1)} %refs_3_.1, ...), custom_call_target="tpu_custom_call" | custom-call | flops 2415919104 | bytes 4718592 | tf_op jit(solution)/shard_map/pallas_call | solution.py:107
  200.6 2.4 %copy.33 = bf16[64,4,12,128]{3,1,0,2:T(4,128)(2,1)} copy(bf16[64,4,12,128]{3,1,2,0:T(4,128)(2,1)} %all-to-all-done.1) | data formatting | bytes 1572864 | tf_op jit(solution)/shard_map/all_to_all | solution.py:169
  203.0 2.4 %copy.30 = bf16[64,4,12,128]{3,1,0,2:T(4,128)(2,1)} copy(bf16[64,4,12,128]{3,1,2,0:T(4,128)(2,1)} %all-to-all-done) | data formatting | bytes 1572864 | tf_op jit(solution)/shard_map/all_to_all | solution.py:169
  205.3 7.1 %shard_map.79 = bf16[12,8,1536]{2,1,0:T(8,128)(2,1)} custom-call(bf16[12,256,128]{2,1,0:T(8,128)(2,1)} %bitcast.100, bf16[12,256,128]{2,1,0:T(8,128)(2,1)} %bitcast.99, bf16[1024,1536]{1,0:T(8,128)(2,1)} %pad_maximum_fusion.refs_2_, bf16[12,16,8,1536]{3,2,1,0:T(8,128)(2,1)} %refs_3_.1, f32[12,8,1536]{2,1,0:T(8,128)} %shard_map.78.refs_4_), custom_call_target="tpu_custom_call" | custom-call | flops 2415919104 | bytes 4718592 | tf_op jit(solution)/shard_map/pallas_call | solution.py:107
  (88 shorter events, 16.8 us)
Async XLA Ops:
  4.3 7.6 %collective-permute-start.6 = (bf16[2,2,2,8,512]{4,3,2,1,0:T(8,128)(2,1)S(1)}, bf16[2,2,2,8,512]{4,3,2,1,0:T(8,128)(2,1)S(1)}, u32[]{:S(2)}, u32[]{:S(2)}) collective-permute-start(bf16[2,2,2,8,512]{4,3,2,1,0:T(8,128)(2,1)S(1)} %get-tuple-element.31), channel_id=1, source_target_pairs={{0,1},{1,2},{2,3},{3,0},{4,5},{5,6},{6,7},{7,4},{8,9},{9,10},{10,1... | collective-permute-start | bytes 196616 | tf_op jit(solution)/shard_map/ppermute | solution.py:165
  6.4 5.6 %collective-permute-start.7 = (bf16[2,2,2,8,512]{4,3,2,1,0:T(8,128)(2,1)S(1)}, bf16[2,2,2,8,512]{4,3,2,1,0:T(8,128)(2,1)S(1)}, u32[]{:S(2)}, u32[]{:S(2)}) collective-permute-start(bf16[2,2,2,8,512]{4,3,2,1,0:T(8,128)(2,1)S(1)} %get-tuple-element.30), channel_id=1, source_target_pairs={{0,2},{1,3},{2,0},{3,1},{4,6},{5,7},{6,4},{7,5},{8,10},{9,11},{10,... | collective-permute-start | bytes 196616 | tf_op jit(solution)/shard_map/ppermute | solution.py:165
  8.8 3.4 %collective-permute-start.8 = (bf16[2,2,2,8,512]{4,3,2,1,0:T(8,128)(2,1)S(1)}, bf16[2,2,2,8,512]{4,3,2,1,0:T(8,128)(2,1)S(1)}, u32[]{:S(2)}, u32[]{:S(2)}) collective-permute-start(bf16[2,2,2,8,512]{4,3,2,1,0:T(8,128)(2,1)S(1)} %get-tuple-element.29), channel_id=1, source_target_pairs={{0,3},{1,0},{2,1},{3,2},{4,7},{5,4},{6,5},{7,6},{8,11},{9,8},{10,9... | collective-permute-start | bytes 196616 | tf_op jit(solution)/shard_map/ppermute | solution.py:165
  11.9 0.6 copy-start.18
  12.0 0.6 copy-start.19
  12.2 0.6 copy-start.20
  12.9 19.8 %copy-start.8 = (bf16[4,32,2,8,512]{4,3,2,1,0:T(8,128)(2,1)S(1)}, bf16[4,32,2,8,512]{4,3,2,1,0:T(8,128)(2,1)}, u32[]{:S(2)}) copy-start(bf16[4,32,2,8,512]{4,3,2,1,0:T(8,128)(2,1)} %param.7) | copy-start | bytes 6291460
  16.8 16.4 %copy-start.21 = (f32[512]{0:T(512)S(1)}, f32[512]{0:T(512)}, u32[]{:S(2)}) copy-start(f32[512]{0:T(512)} %param.9) | copy-start | bytes 6148
  19.0 29.1 %all-to-all-start.2 = ((bf16[64,2,12,128]{3,1,2,0:T(2,128)(2,1)}), bf16[64,2,12,128]{3,1,2,0:T(2,128)(2,1)S(1)}, u32[]{:S(2)}, u32[]{:S(2)}) async-start(bf16[64,2,12,128]{3,1,2,0:T(2,128)(2,1)} %copy.35), calls=%async_computation.2 | async-start | bytes 786432 | tf_op jit(solution)/shard_map/all_to_all | solution.py:169
  34.2 5.1 %collective-permute-start.12 = (bf16[2,2,3,8,512]{4,3,2,1,0:T(8,128)(2,1)S(1)}, bf16[2,2,3,8,512]{4,3,2,1,0:T(8,128)(2,1)S(1)}, u32[]{:S(2)}, u32[]{:S(2)}) collective-permute-start(bf16[2,2,3,8,512]{4,3,2,1,0:T(8,128)(2,1)S(1)} %get-tuple-element.23), channel_id=1, source_target_pairs={{0,1},{1,2},{2,3},{3,0},{4,5},{5,6},{6,7},{7,4},{8,9},{9,10},{10,1... | collective-permute-start | bytes 294920 | tf_op jit(solution)/shard_map/ppermute | solution.py:165
  34.5 7.8 %collective-permute-start.13 = (bf16[2,2,3,8,512]{4,3,2,1,0:T(8,128)(2,1)S(1)}, bf16[2,2,3,8,512]{4,3,2,1,0:T(8,128)(2,1)S(1)}, u32[]{:S(2)}, u32[]{:S(2)}) collective-permute-start(bf16[2,2,3,8,512]{4,3,2,1,0:T(8,128)(2,1)S(1)} %get-tuple-element.22), channel_id=1, source_target_pairs={{0,2},{1,3},{2,0},{3,1},{4,6},{5,7},{6,4},{7,5},{8,10},{9,11},{10,... | collective-permute-start | bytes 294920 | tf_op jit(solution)/shard_map/ppermute | solution.py:165
  37.8 4.5 %collective-permute-start.14 = (bf16[2,2,3,8,512]{4,3,2,1,0:T(8,128)(2,1)S(1)}, bf16[2,2,3,8,512]{4,3,2,1,0:T(8,128)(2,1)S(1)}, u32[]{:S(2)}, u32[]{:S(2)}) collective-permute-start(bf16[2,2,3,8,512]{4,3,2,1,0:T(8,128)(2,1)S(1)} %get-tuple-element.21), channel_id=1, source_target_pairs={{0,3},{1,0},{2,1},{3,2},{4,7},{5,4},{6,5},{7,6},{8,11},{9,8},{10,9... | collective-permute-start | bytes 294920 | tf_op jit(solution)/shard_map/ppermute | solution.py:165
  39.3 3.0 %copy-start.12 = (bf16[2,2,3,8,512]{4,3,2,1,0:T(8,128)(2,1)}, bf16[2,2,3,8,512]{4,3,2,1,0:T(8,128)(2,1)S(1)}, u32[]{:S(2)}) copy-start(bf16[2,2,3,8,512]{4,3,2,1,0:T(8,128)(2,1)S(1)} %collective-permute-done.12.refs_1_) | copy-start | bytes 294916
  42.3 0.6 copy-start.14
  42.3 0.7 copy-start.16
  48.1 34.2 %all-to-all-start.4 = ((bf16[64,3,12,128]{3,2,1,0:T(8,128)(2,1)}), bf16[64,3,12,128]{3,2,1,0:T(8,128)(2,1)S(1)}, u32[]{:S(2)}, u32[]{:S(2)}) async-start(bf16[64,3,12,128]{3,2,1,0:T(8,128)(2,1)} %shard_map.77), calls=%async_computation.4 | async-start | bytes 1572864 | tf_op jit(solution)/shard_map/all_to_all | solution.py:169
  60.3 5.4 %collective-permute-start.10 = (bf16[2,2,3,8,512]{4,3,2,1,0:T(8,128)(2,1)S(1)}, bf16[2,2,3,8,512]{4,3,2,1,0:T(8,128)(2,1)S(1)}, u32[]{:S(2)}, u32[]{:S(2)}) collective-permute-start(bf16[2,2,3,8,512]{4,3,2,1,0:T(8,128)(2,1)S(1)} %get-tuple-element.26), channel_id=1, source_target_pairs={{0,2},{1,3},{2,0},{3,1},{4,6},{5,7},{6,4},{7,5},{8,10},{9,11},{10,... | collective-permute-start | bytes 294920 | tf_op jit(solution)/shard_map/ppermute | solution.py:165
  61.3 6.2 %collective-permute-start.11 = (bf16[2,2,3,8,512]{4,3,2,1,0:T(8,128)(2,1)S(1)}, bf16[2,2,3,8,512]{4,3,2,1,0:T(8,128)(2,1)S(1)}, u32[]{:S(2)}, u32[]{:S(2)}) collective-permute-start(bf16[2,2,3,8,512]{4,3,2,1,0:T(8,128)(2,1)S(1)} %get-tuple-element.25), channel_id=1, source_target_pairs={{0,3},{1,0},{2,1},{3,2},{4,7},{5,4},{6,5},{7,6},{8,11},{9,8},{10,9... | collective-permute-start | bytes 294920 | tf_op jit(solution)/shard_map/ppermute | solution.py:165
  63.1 5.1 %collective-permute-start.9 = (bf16[2,2,3,8,512]{4,3,2,1,0:T(8,128)(2,1)S(1)}, bf16[2,2,3,8,512]{4,3,2,1,0:T(8,128)(2,1)S(1)}, u32[]{:S(2)}, u32[]{:S(2)}) collective-permute-start(bf16[2,2,3,8,512]{4,3,2,1,0:T(8,128)(2,1)S(1)} %get-tuple-element.27), channel_id=1, source_target_pairs={{0,1},{1,2},{2,3},{3,0},{4,5},{5,6},{6,7},{7,4},{8,9},{9,10},{10,1... | collective-permute-start | bytes 294920 | tf_op jit(solution)/shard_map/ppermute | solution.py:165
  65.7 2.5 %copy-start.13 = (bf16[2,2,3,8,512]{4,3,2,1,0:T(8,128)(2,1)}, bf16[2,2,3,8,512]{4,3,2,1,0:T(8,128)(2,1)S(1)}, u32[]{:S(2)}) copy-start(bf16[2,2,3,8,512]{4,3,2,1,0:T(8,128)(2,1)S(1)} %collective-permute-done.10.refs_2_) | copy-start | bytes 294916
  67.5 0.7 copy-start.15
  68.2 0.6 copy-start.17
  82.3 12.6 %copy-start.4 = (bf16[64,3,12,128]{3,2,1,0:T(8,128)(2,1)}, bf16[64,3,12,128]{3,2,1,0:T(8,128)(2,1)S(1)}, u32[]{:S(2)}) copy-start(bf16[64,3,12,128]{3,2,1,0:T(8,128)(2,1)S(1)} %all-to-all-done.4) | copy-start | bytes 1769476
  82.3 28.9 %all-to-all-start.3 = ((bf16[64,3,12,128]{3,2,1,0:T(8,128)(2,1)}), bf16[64,3,12,128]{3,2,1,0:T(8,128)(2,1)S(1)}, u32[]{:S(2)}, u32[]{:S(2)}) async-start(bf16[64,3,12,128]{3,2,1,0:T(8,128)(2,1)} %shard_map.76), calls=%async_computation.3 | async-start | bytes 1572864 | tf_op jit(solution)/shard_map/all_to_all | solution.py:169
  91.4 5.8 %collective-permute-start.3 = (bf16[2,2,4,8,512]{4,3,2,1,0:T(8,128)(2,1)S(1)}, bf16[2,2,4,8,512]{4,3,2,1,0:T(8,128)(2,1)S(1)}, u32[]{:S(2)}, u32[]{:S(2)}) collective-permute-start(bf16[2,2,4,8,512]{4,3,2,1,0:T(8,128)(2,1)S(1)} %get-tuple-element.15), channel_id=1, source_target_pairs={{0,1},{1,2},{2,3},{3,0},{4,5},{5,6},{6,7},{7,4},{8,9},{9,10},{10,1... | collective-permute-start | bytes 393224 | tf_op jit(solution)/shard_map/ppermute | solution.py:165
  91.7 8.8 %collective-permute-start.4 = (bf16[2,2,4,8,512]{4,3,2,1,0:T(8,128)(2,1)S(1)}, bf16[2,2,4,8,512]{4,3,2,1,0:T(8,128)(2,1)S(1)}, u32[]{:S(2)}, u32[]{:S(2)}) collective-permute-start(bf16[2,2,4,8,512]{4,3,2,1,0:T(8,128)(2,1)S(1)} %get-tuple-element.14), channel_id=1, source_target_pairs={{0,2},{1,3},{2,0},{3,1},{4,6},{5,7},{6,4},{7,5},{8,10},{9,11},{10,... | collective-permute-start | bytes 393224 | tf_op jit(solution)/shard_map/ppermute | solution.py:165
  94.6 5.9 %collective-permute-start.5 = (bf16[2,2,4,8,512]{4,3,2,1,0:T(8,128)(2,1)S(1)}, bf16[2,2,4,8,512]{4,3,2,1,0:T(8,128)(2,1)S(1)}, u32[]{:S(2)}, u32[]{:S(2)}) collective-permute-start(bf16[2,2,4,8,512]{4,3,2,1,0:T(8,128)(2,1)S(1)} %get-tuple-element.13), channel_id=1, source_target_pairs={{0,3},{1,0},{2,1},{3,2},{4,7},{5,4},{6,5},{7,6},{8,11},{9,8},{10,9... | collective-permute-start | bytes 393224 | tf_op jit(solution)/shard_map/ppermute | solution.py:165
  97.2 3.4 %copy-start.9 = (bf16[2,2,4,8,512]{4,3,2,1,0:T(8,128)(2,1)}, bf16[2,2,4,8,512]{4,3,2,1,0:T(8,128)(2,1)S(1)}, u32[]{:S(2)}) copy-start(bf16[2,2,4,8,512]{4,3,2,1,0:T(8,128)(2,1)S(1)} %collective-permute-done.3.refs_1_) | copy-start | bytes 393220
  100.6 0.7 copy-start.10
  100.6 0.7 copy-start.11
  107.2 18.2 %copy-start.22 = (s32[512]{0:T(512)S(1)}, s32[512]{0:T(512)}, u32[]{:S(2)}) copy-start(s32[512]{0:T(512)} %param.11) | copy-start | bytes 6148
  111.3 15.5 %copy-start.6 = (bf16[64,3,12,128]{3,2,1,0:T(8,128)(2,1)}, bf16[64,3,12,128]{3,2,1,0:T(8,128)(2,1)S(1)}, u32[]{:S(2)}) copy-start(bf16[64,3,12,128]{3,2,1,0:T(8,128)(2,1)S(1)} %all-to-all-done.3) | copy-start | bytes 1769476
  111.3 42.0 %all-to-all-start.1 = ((bf16[64,4,12,128]{3,1,2,0:T(4,128)(2,1)}), bf16[64,4,12,128]{3,1,2,0:T(4,128)(2,1)}, u32[]{:S(2)}, u32[]{:S(2)}) async-start(bf16[64,4,12,128]{3,1,2,0:T(4,128)(2,1)} %copy.32), calls=%async_computation.1 | async-start | bytes 1572864 | tf_op jit(solution)/shard_map/all_to_all | solution.py:169
  121.8 23.0 %collective-permute-start = (bf16[2,2,4,8,512]{4,3,2,1,0:T(8,128)(2,1)}, bf16[2,2,4,8,512]{4,3,2,1,0:T(8,128)(2,1)}, u32[]{:S(2)}, u32[]{:S(2)}) collective-permute-start(bf16[2,2,4,8,512]{4,3,2,1,0:T(8,128)(2,1)} %get-tuple-element.19), channel_id=1, source_target_pairs={{0,1},{1,2},{2,3},{3,0},{4,5},{5,6},{6,7},{7,4},{8,9},{9,10},{10,1... | collective-permute-start | bytes 393224 | tf_op jit(solution)/shard_map/ppermute | solution.py:165
  122.1 22.7 %collective-permute-start.1 = (bf16[2,2,4,8,512]{4,3,2,1,0:T(8,128)(2,1)}, bf16[2,2,4,8,512]{4,3,2,1,0:T(8,128)(2,1)}, u32[]{:S(2)}, u32[]{:S(2)}) collective-permute-start(bf16[2,2,4,8,512]{4,3,2,1,0:T(8,128)(2,1)} %get-tuple-element.18), channel_id=1, source_target_pairs={{0,2},{1,3},{2,0},{3,1},{4,6},{5,7},{6,4},{7,5},{8,10},{9,11},{10,... | collective-permute-start | bytes 393224 | tf_op jit(solution)/shard_map/ppermute | solution.py:165
  125.4 19.5 %collective-permute-start.2 = (bf16[2,2,4,8,512]{4,3,2,1,0:T(8,128)(2,1)}, bf16[2,2,4,8,512]{4,3,2,1,0:T(8,128)(2,1)}, u32[]{:S(2)}, u32[]{:S(2)}) collective-permute-start(bf16[2,2,4,8,512]{4,3,2,1,0:T(8,128)(2,1)} %get-tuple-element.17), channel_id=1, source_target_pairs={{0,3},{1,0},{2,1},{3,2},{4,7},{5,4},{6,5},{7,6},{8,11},{9,8},{10,9... | collective-permute-start | bytes 393224 | tf_op jit(solution)/shard_map/ppermute | solution.py:165
  153.3 49.7 %all-to-all-start = ((bf16[64,4,12,128]{3,1,2,0:T(4,128)(2,1)}), bf16[64,4,12,128]{3,1,2,0:T(4,128)(2,1)}, u32[]{:S(2)}, u32[]{:S(2)}) async-start(bf16[64,4,12,128]{3,1,2,0:T(4,128)(2,1)} %copy.29), calls=%async_computation | async-start | bytes 1572864 | tf_op jit(solution)/shard_map/all_to_all | solution.py:169
  179.7 2.9 %copy-start = (bf16[2,64,4,1536]{3,2,1,0:T(4,128)(2,1)S(1)}, bf16[2,64,4,1536]{3,2,1,0:T(4,128)(2,1)}, u32[]{:S(2)}) copy-start(bf16[2,64,4,1536]{3,2,1,0:T(4,128)(2,1)} %get-tuple-element.8) | copy-start | bytes 4718596
  183.9 3.4 %copy-start.1 = (bf16[384,1536]{1,0:T(8,128)(2,1)S(1)}, bf16[384,1536]{1,0:T(8,128)(2,1)}, u32[]{:S(2)}) copy-start(bf16[384,1536]{1,0:T(8,128)(2,1)} %reshape.203) | copy-start | bytes 3538948
  183.9 3.4 %copy-start.2 = (bf16[384,1536]{1,0:T(8,128)(2,1)S(1)}, bf16[384,1536]{1,0:T(8,128)(2,1)}, u32[]{:S(2)}) copy-start(bf16[384,1536]{1,0:T(8,128)(2,1)} %reshape.204) | copy-start | bytes 3538948
  183.9 3.4 %copy-start.3 = (bf16[256,1536]{1,0:T(8,128)(2,1)S(1)}, bf16[256,1536]{1,0:T(8,128)(2,1)}, u32[]{:S(2)}) copy-start(bf16[256,1536]{1,0:T(8,128)(2,1)} %reshape.202) | copy-start | bytes 2359300
  187.3 3.0 %copy-start.5 = (bf16[64,3,12,128]{3,2,1,0:T(8,128)(2,1)S(1)}, bf16[64,3,12,128]{3,2,1,0:T(8,128)(2,1)}, u32[]{:S(2)}) copy-start(bf16[64,3,12,128]{3,2,1,0:T(8,128)(2,1)} %copy-done.4) | copy-start | bytes 1769476
  187.3 4.0 %copy-start.7 = (bf16[64,3,12,128]{3,2,1,0:T(8,128)(2,1)S(1)}, bf16[64,3,12,128]{3,2,1,0:T(8,128)(2,1)}, u32[]{:S(2)}) copy-start(bf16[64,3,12,128]{3,2,1,0:T(8,128)(2,1)} %copy-done.6) | copy-start | bytes 1769476
where the time goes:
time: 214 us; the launch traced here: 212 us
  starting transfers between devices  70.4 us (33%)
  local copies, waits for them, and re-layouts  43.3 us (20%)
  Pallas kernels  41 us (19%)
  other arithmetic  29.8 us (14%)
  waiting for transfers between devices  25.5 us (12%)
  matrix products  2.29 us (1%)
    all_to_all x5, starting transfers between devices, shards(): four = lax.all_to_all(four, 'rows', split_axis=0, concat_axis=0, tiled=True)  51.7 us
    pallas_call x5, Pallas kernels, legendre_step(): pl.pallas_call(legendre_kernel, grid=(slots,), out_shape=jax.ShapeDtypeSt...  26.1 us
    ppermute x15, starting transfers between devices, shards(): lax.ppermute(spec[i], 'mem', [(d, (d + i) % mem_count) for d in range(mem...  18.7 us
    ppermute x15, waiting for transfers between devices, shards(): lax.ppermute(spec[i], 'mem', [(d, (d + i) % mem_count) for d in range(mem...  15.5 us
    reshape x5, local copies, waits for them, and re-layouts, ordered_basis(): pieces.append(basis[:, :, first:first + slots].reshape(-1, lon_count))  15.1 us
    pallas_call x2, Pallas kernels, zonal_step(): pl.pallas_call(functools.partial(zonal_kernel, len(fours), half), grid=(l...  14.8 us
    another operation x1, other arithmetic  14.5 us
    all_to_all x5, waiting for transfers between devices, shards(): four = lax.all_to_all(four, 'rows', split_axis=0, concat_axis=0, tiled=True)  10 us
  transfers between devices with their start and end apart: 20, of which 10 were waited for; matrix products, arithmetic and copies ran while one was open for 30% of the time, Pallas kernels for 14%

commit v1 on v0

v1 whole, which is shorter than its diff:
```python
import functools
import math

import jax
import jax.numpy as jnp
from jax import lax
from jax.experimental import pallas as pl
from jax.experimental.pallas import tpu as pltpu
from jax.sharding import PartitionSpec as P

HALVES = 2
QUADS = 2
LATS = 4
LANES = 128
PIECE = 512
VMEM_LIMIT = 60 * 1024 * 1024
MESH = pl.DeviceIdType.MESH
Z, Y, CORES = 8, 4, 2


def f32(x):
    return x.astype(jnp.float32)


def bf16(x):
    return x.astype(jnp.bfloat16)


def iota(shape, dim):
    return lax.broadcasted_iota(jnp.int32, shape, dim)


def peer(rows, step):
    z, y, c = rows // (Y * CORES), (rows // CORES) % Y, rows % CORES
    k, w = step // (Y * CORES), step % (Y * CORES)
    dz = Z // 2 + (1 - 2 * (k % 2)) * ((k + 1) // 2)
    z = lax.rem(z + dz, Z)
    y = lax.rem(y + w // CORES + 1, Y)
    c = lax.rem(c + w + 1, CORES)
    return (z * Y + y) * CORES + c


def kernel(
    root_ref, loc_ref, order_ref, wave_ref, ctl_hbm, leg_hbm, ptb_hbm, out_ref,
    ctl, leg, ptb, kron, onehot, sx, rx, stage, sbuf, gbuf, basis, part,
    load_sem, xs_sem, xr_sem, as_sem, ar_sem, own_sem,
):
    rows = lax.axis_index("rows")
    me = lax.axis_index("mem")
    mem_count, row_count = 4, 64
    members, modes, _, slots, totals = ctl.shape
    taken = members // HALVES
    levels = modes // mem_count
    lat_count = leg.shape[2]
    quad = slots // QUADS
    tall = taken * levels

    barrier = pltpu.get_barrier_semaphore()

    def greet(step, carry):
        pl.semaphore_signal(barrier, inc=1, device_id=(peer(rows, step), me), device_id_type=MESH)
        return carry

    for i in range(1, mem_count):
        pl.semaphore_signal(
            barrier, inc=1, device_id=(rows, lax.rem(me + i, mem_count)), device_id_type=MESH
        )
    lax.fori_loop(0, row_count - 1, greet, 0)

    ctl_in = [
        pltpu.make_async_copy(
            ctl_hbm.at[pl.ds(h * taken, taken)], ctl.at[pl.ds(h * taken, taken)], load_sem.at[h]
        )
        for h in range(HALVES)
    ]
    leg_in = pltpu.make_async_copy(leg_hbm, leg, load_sem.at[2])
    ptb_in = pltpu.make_async_copy(ptb_hbm, ptb, load_sem.at[3])
    for c in ctl_in:
        c.start()
    leg_in.start()
    ptb_in.start()

    size = slots * taken * modes
    row, col = iota((size, modes), 0), iota((size, modes), 1)
    level = lax.rem(me + row // (slots * tall), mem_count) * levels + row % levels
    pick = bf16(f32(level == col))
    spread = bf16(f32(iota((modes, size), 0) == (iota((modes, size), 1) // slots) % modes))
    wide = jnp.dot(pick, bf16(root_ref[...]), preferred_element_type=jnp.float32)
    wide = jnp.dot(bf16(wide), spread, preferred_element_type=jnp.float32)
    row, col = iota((size, size), 0), iota((size, size), 1)
    same = ((row // tall) % slots == col % slots) & ((row // levels) % taken == col // (modes * slots))
    kron[...] = bf16(jnp.where(same, wide, 0.0))

    def spectra(h):
        ctl_in[h].wait()
        for r in range(2):
            x = f32(ctl[h * taken : (h + 1) * taken, :, r])
            x = bf16(x.reshape(taken * modes * slots, totals))
            spec = jnp.dot(kron[...], x, preferred_element_type=jnp.float32) * loc_ref[...]
            spec = bf16(spec).reshape(mem_count, slots, tall, totals)
            sx[h, :, :, r] = spec
            rx[h, 0, :, r] = spec[0]

    def exchange(h, q, i):
        part_of = pl.ds(q * quad, quad)
        return pltpu.make_async_remote_copy(
            src_ref=sx.at[h, i, part_of],
            dst_ref=rx.at[h, i, part_of],
            send_sem=xs_sem,
            recv_sem=xr_sem.at[h * QUADS + q],
            device_id=(rows, lax.rem(me + i, mem_count)),
            device_id_type=MESH,
        )

    spectra(0)
    pl.semaphore_wait(barrier, row_count + mem_count - 2)
    for q in range(QUADS):
        for i in range(1, mem_count):
            exchange(0, q, i).start()
    spectra(1)
    for q in range(QUADS):
        for i in range(1, mem_count):
            exchange(1, q, i).start()

    onehot[...] = bf16(f32(iota((lat_count, lat_count), 0) == order_ref[...])).T
    leg_in.wait()

    def wait_exchange(hq):
        h, q = hq // QUADS, hq % QUADS
        got = rx.at[h, pl.ds(1, mem_count - 1), pl.ds(q * quad, quad)]
        pltpu.make_async_copy(got, got, xr_sem.at[hq]).wait()

    def send(hq, b, dest, sem):
        lo, n = ((0, 32), (32, 16))[b]
        return pltpu.make_async_remote_copy(
            src_ref=sbuf.at[hq, dest, pl.ds(lo, n)],
            dst_ref=gbuf.at[hq, rows, pl.ds(lo, n)],
            send_sem=as_sem,
            recv_sem=sem,
            device_id=(dest, me),
            device_id_type=MESH,
        )

    def legendre_step(hq, carry):
        h, q = hq // QUADS, hq % QUADS
        wait_exchange(hq)
        for s in range(quad):
            x = rx[h, :, q * quad + s]
            x = jnp.concatenate([x[:, r].reshape(mem_count * tall, totals) for r in range(2)], axis=0)
            four = bf16(jnp.dot(x, leg[q * quad + s], preferred_element_type=jnp.float32))
            stage[pl.ds(s, lat_count, stride=quad), :] = lax.dot_general(
                onehot[...], four, (((1,), (1,)), ((), ())), preferred_element_type=jnp.float32
            )
        sbuf[hq] = bf16(stage[...]).reshape(row_count, lat_count * quad // row_count, LANES)
        pltpu.make_async_copy(sbuf.at[hq, rows], gbuf.at[hq, rows], own_sem).start()
        for b in range(2):
            def push(step, c):
                send(hq, b, peer(rows, step), ar_sem.at[hq * 2 + b]).start()
                return c
            lax.fori_loop(0, row_count - 1, push, 0)
        return carry

    lax.fori_loop(0, HALVES * QUADS, legendre_step, 0)

    slot_count, lon_count = basis.shape[0] // 2, basis.shape[1]
    wave = jnp.broadcast_to(wave_ref[...], (LANES, slot_count)).T
    weight = jnp.where(wave == 0, 1.0, 2.0)
    angle = f32(lax.rem(wave * iota((slot_count, LANES), 1), lon_count)) * (2.0 * math.pi / lon_count)
    fine_cos, fine_sin = weight * jnp.cos(angle), weight * jnp.sin(angle)
    turns = lon_count // LANES
    angle = f32(lax.rem(wave * iota((slot_count, LANES), 1), turns)) * (2.0 * math.pi / turns)
    wide_cos, wide_sin = jnp.cos(angle), jnp.sin(angle)
    for a in range(turns):
        x = pl.ds(a * LANES, LANES)
        wc = wide_cos[:, a : a + 1]
        ws = wide_sin[:, a : a + 1]
        basis[pl.ds(0, slot_count), x] = bf16(fine_cos * wc - fine_sin * ws)
        basis[pl.ds(slot_count, slot_count), x] = bf16(-(fine_sin * wc + fine_cos * ws))

    part[...] = jnp.zeros_like(part)
    ptb_in.wait()
    for hq in range(HALVES * QUADS):
        pltpu.make_async_copy(sbuf.at[hq, 0], gbuf.at[hq, 0], own_sem).wait()

    def arrived(hq, b):
        lo, n = ((0, 32), (32, 16))[b]
        got = gbuf.at[hq, pl.ds(0, row_count - 1), pl.ds(lo, n)]
        pltpu.make_async_copy(got, got, ar_sem.at[hq * 2 + b]).wait()

    upper = iota((row_count, 2 * quad, LANES), 1) >= quad

    def zonal_step(t, carry):
        h, b = t // 3, t % 3

        @pl.when(t == 0)
        def _():
            for hq in range(2):
                arrived(hq, 0)
                arrived(hq, 1)

        @pl.when(t == 3)
        def _():
            arrived(2, 0)
            arrived(3, 0)

        @pl.when(t == 5)
        def _():
            arrived(2, 1)
            arrived(3, 1)

        tile = pl.ds(pl.multiple_of(b * 16, 16), 16)
        first = f32(gbuf[h * QUADS, :, tile, :])
        second = f32(gbuf[h * QUADS + 1, :, tile, :])
        blocks = []
        for p in range(LATS // 2):
            u = first[:, p * 8 : p * 8 + 8]
            v = second[:, p * 8 : p * 8 + 8]
            for got in (
                jnp.where(upper, pltpu.roll(v, quad, 1), u),
                jnp.where(upper, v, pltpu.roll(u, quad, 1)),
            ):
                pair = bf16(got.reshape(row_count * slots, LANES)).T
                blocks.append(jnp.concatenate([pair[: LANES // 2], pair[LANES // 2 :]], axis=1))
        lhs = jnp.concatenate(blocks, axis=0)
        lats = pl.ds(b * LATS, LATS)
        for x in range(0, lon_count, PIECE):
            field = jnp.dot(lhs, basis[:, x : x + PIECE], preferred_element_type=jnp.float32)
            field = f32(bf16(field)).reshape(LATS, mem_count, taken, levels, PIECE)
            total = part[lats, :, x : x + PIECE]
            for i in range(mem_count):
                source = lax.rem(me + mem_count - i, mem_count)
                begin = source * members + h * taken
                near = f32(ptb[lats, pl.ds(begin, taken), :, x : x + PIECE])
                total += jnp.sum(field[:, i] * near, axis=1)
            part[lats, :, x : x + PIECE] = total
            out_ref[lats, :, x : x + PIECE] = bf16(total)
        return carry

    lax.fori_loop(0, HALVES * 3, zonal_step, 0)

    sent = sx.at[:, pl.ds(1, mem_count - 1)]
    pltpu.make_async_copy(sent, sent, xs_sem).wait()
    sent = sbuf.at[:, pl.ds(0, row_count - 1)]
    pltpu.make_async_copy(sent, sent, as_sem).wait()


def shards(control, vert_root, loc_spec, legendre, wave_table, lat_order, perturb):
    members, modes, parts, slots, totals = control.shape
    lat_count = legendre.shape[2]
    lats, _, levels, lon_count = perturb.shape
    row_count, mem_count = 64, 4
    taken = members // HALVES
    tall = taken * levels
    quad = slots // QUADS
    each = lats * quad
    size = slots * taken * modes
    small = pl.BlockSpec(memory_space=pltpu.VMEM)
    large = pl.BlockSpec(memory_space=pl.ANY)
    half = jnp.bfloat16
    return pl.pallas_call(
        kernel,
        out_shape=jax.ShapeDtypeStruct((lats, levels, lon_count), half),
        in_specs=[small, small, small, small, large, large, large],
        out_specs=small,
        scratch_shapes=[
            pltpu.VMEM(control.shape, half),
            pltpu.VMEM(legendre.shape, half),
            pltpu.VMEM(perturb.shape, half),
            pltpu.VMEM((size, size), half),
            pltpu.VMEM((lat_count, lat_count), half),
            pltpu.VMEM((HALVES, mem_count, slots, parts, tall, totals), half),
            pltpu.VMEM((HALVES, mem_count, slots, parts, tall, totals), half),
            pltpu.VMEM((lat_count * quad, LANES), jnp.float32),
            pltpu.VMEM((HALVES * QUADS, row_count, each, LANES), half),
            pltpu.VMEM((HALVES * QUADS, row_count, each, LANES), half),
            pltpu.VMEM((2 * row_count * slots, lon_count), half),
            pltpu.VMEM((lats, levels, lon_count), jnp.float32),
            pltpu.SemaphoreType.DMA((4,)),
            pltpu.SemaphoreType.DMA,
            pltpu.SemaphoreType.DMA((HALVES * QUADS,)),
            pltpu.SemaphoreType.DMA,
            pltpu.SemaphoreType.DMA((HALVES * QUADS * 2,)),
            pltpu.SemaphoreType.DMA,
        ],
        compiler_params=pltpu.CompilerParams(
            collective_id=0, has_side_effects=True, vmem_limit_bytes=VMEM_LIMIT
        ),
    )(
        vert_root,
        loc_spec[None],
        lat_order[None],
        wave_table[None],
        control,
        legendre,
        perturb,
    )


def solution(mesh):
    return jax.shard_map(
        shards,
        mesh=mesh,
        in_specs=(
            P("mem", None, None, "rows", None),
            P(),
            P(),
            P("rows", None, None),
            P(),
            P(),
            P("rows", None, "mem", None),
        ),
        out_specs=P("rows", "mem", None),
        check_vma=False,
    )
```

time: 214 us -> 98.7 us (0.46)
  starting transfers between devices: 70.4 us -> 0 us
  Pallas kernels: 41 us -> 95.6 us
  local copies, waits for them, and re-layouts: 43.3 us -> 2.96 us
  other arithmetic: 29.8 us -> 0 us
  waiting for transfers between devices: 25.5 us -> 0 us
  matrix products: 2.29 us -> 0 us
    pallas_call x7 -> x1, Pallas kernels: 41 us -> 95.6 us  [shards(): pl.pallas_call(kernel, out_shape=jax.ShapeDtypeStruct((lats, levels, lon_...]
    all_to_all x5 -> x0, starting transfers between devices: 51.7 us -> none  [shards(): four = lax.all_to_all(four, 'rows', split_axis=0, concat_axis=0, tiled=True)]
    another operation x4 -> x0, other arithmetic: 21.8 us -> none
    ppermute x15 -> x0, starting transfers between devices: 18.7 us -> none  [shards(): lax.ppermute(spec[i], 'mem', [(d, (d + i) % mem_count) for d in range(mem...]
    reshape x7 -> x0, local copies, waits for them, and re-layouts: 17.1 us -> none  [the longest x5 15.1 us: ordered_basis(): pieces.append(basis[:, :, first:first + slots].reshape(-1, lon_count))]
    ppermute x15 -> x0, waiting for transfers between devices: 15.5 us -> none  [shards(): lax.ppermute(spec[i], 'mem', [(d, (d + i) % mem_count) for d in range(mem...]
    all_to_all x5 -> x0, waiting for transfers between devices: 10 us -> none  [shards(): four = lax.all_to_all(four, 'rows', split_axis=0, concat_axis=0, tiled=True)]
    pallas_call x3 -> x0, local copies, waits for them, and re-layouts: 6.96 us -> none  [legendre_step(): pl.pallas_call(legendre_kernel, grid=(slots,), out_shape=jax.ShapeDtypeSt...]
  transfers between devices with their start and end apart: 20 -> 0, of which waited for: 10 -> 0; matrix products, arithmetic and copies ran while one was open for 30% -> 0% of each run, Pallas kernels for 14% -> 0%
where the time goes in v1:
time: 98.7 us; the launch traced here: 98.5 us
  Pallas kernels  95.6 us (97%)
  local copies, waits for them, and re-layouts  2.96 us (3%)
    pallas_call x1, Pallas kernels, shards(): pl.pallas_call(kernel, out_shape=jax.ShapeDtypeStruct((lats, levels, lon_...  95.6 us

profile of v1, /device:TPU:1, one launch (start us, length us, event | category | flops | bytes accessed | tf_op | source)
XLA Modules:
  0.0 98.5 jit_solution(2952452128864834398)
XLA Ops:
  0.0 1.3 %broadcast_in_dim.10.order_ref = s32[1,768]{1,0:T(1,128)} reshape(s32[768]{0:T(1024)} %param.12) | data formatting | bytes 6144 | tf_op jit(solution)/shard_map/broadcast_in_dim | solution.py:291
  1.3 95.6 %shard_map.73 = bf16[12,8,1536]{2,1,0:T(8,128)(2,1)} custom-call(f32[32,32]{1,0:T(8,128)} %root_ref.1, f32[1,512]{1,0:T(1,128)} %bitcast.2, s32[1,768]{1,0:T(1,128)} %broadcast_in_dim.10.order_ref, s32[1,512]{1,0:T(1,128)} %bitcast.3, bf16[4,32,2,8,512]{4,3,2,1,0:T(8,128)(2,1)} %ctl_hbm.1, bf16[8,512,768]{2,1,0:T(8,128)(2,1)} %leg_hbm.1, ...), custom_call_target="tpu_custom_call" | custom-call | tf_op jit(solution)/shard_map/pallas_call | solution.py:260
  96.8 1.7 %copy.9 = bf16[12,8,1536]{2,1,0:T(8,128)(2,1)} copy(bf16[12,8,1536]{2,1,0:T(8,128)(2,1)} %shard_map.73) | data formatting | bytes 589824

commit v2 on v1

v2 whole, which is shorter than its diff:
```python
import functools
import math

import jax
import jax.numpy as jnp
from jax import lax
from jax.experimental import pallas as pl
from jax.experimental.pallas import tpu as pltpu
from jax.sharding import PartitionSpec as P

HALVES = 2
QUADS = 2
LATS = 4
LANES = 128
PIECE = 512
OWN, SIDES, FAR = 0, 1, 3
CHUNKS = 4
PARTS = ((0, 48), (0, 48), (0, 48), (0, 32), (32, 16))
VMEM_LIMIT = 60 * 1024 * 1024
MESH = pl.DeviceIdType.MESH
Z, Y, CORES = 8, 4, 2


def f32(x):
    return x.astype(jnp.float32)


def bf16(x):
    return x.astype(jnp.bfloat16)


def iota(shape, dim):
    return lax.broadcasted_iota(jnp.int32, shape, dim)


def turn(at, by, count):
    return lax.rem(at + by, count)


def unweave(x, slots):
    half, both = x.shape[0] // 2, x.shape[1]
    upper = iota((half, both, x.shape[2]), 1) >= slots
    near, far = x[:half], x[half:]
    first = jnp.where(upper, pltpu.roll(far, slots, 1), near)
    second = jnp.where(upper, far, pltpu.roll(near, slots, 1))
    return [v.reshape(half * both, x.shape[2]) for v in (first, second)]


def kernel(
    root_ref, loc_ref, order_ref, wave_ref, ctl_hbm, leg_hbm, ptb_hbm, out_ref,
    ctl, leg, ptb, kron, onehot, sx, rx, stage, sbuf, gbuf, basis, total,
    load_sem, xs_sem, xr_sem, as_sem, ar_sem, own_sem,
):
    rows = lax.axis_index("rows")
    me = lax.axis_index("mem")
    mem_count, row_count = 4, 64
    members, modes, _, slots, totals = ctl.shape
    taken = members // HALVES
    levels = modes // mem_count
    lat_count = leg.shape[2]
    quad = slots // QUADS
    tall = taken * levels
    lats = lat_count // row_count

    ctl_in = [
        pltpu.make_async_copy(
            ctl_hbm.at[pl.ds(h * taken, taken)], ctl.at[pl.ds(h * taken, taken)], load_sem.at[h]
        )
        for h in range(HALVES)
    ]
    leg_in = pltpu.make_async_copy(leg_hbm, leg, load_sem.at[2])
    ptb_in = pltpu.make_async_copy(ptb_hbm, ptb, load_sem.at[3])
    for c in ctl_in:
        c.start()
    leg_in.start()

    barrier = pltpu.get_barrier_semaphore()
    z, y, core = rows // (Y * CORES), (rows // CORES) % Y, rows % CORES
    spots = [
        turn(y, w // CORES + 1, Y) * CORES + turn(core, w + 1, CORES) for w in range(Y * CORES)
    ]

    def each_peer(act):
        def plane(k, carry):
            dz = Z // 2 + (1 - 2 * (k % 2)) * ((k + 1) // 2)
            base = turn(z, dz, Z) * (Y * CORES)
            for spot in spots:
                act(base + spot)
            return carry

        lax.fori_loop(0, Z - 1, plane, 0)
        for spot in spots[:-1]:
            act(z * (Y * CORES) + spot)

    def greet(dest):
        pl.semaphore_signal(barrier, inc=1, device_id=(dest, me), device_id_type=MESH)

    each_peer(greet)
    for i in range(1, mem_count):
        pl.semaphore_signal(
            barrier, inc=1, device_id=(rows, turn(me, i, mem_count)), device_id_type=MESH
        )

    size = slots * taken * modes
    row, col = iota((size, modes), 0), iota((size, modes), 1)
    level = lax.rem(me + row // (slots * tall), mem_count) * levels + row % levels
    pick = bf16(f32(level == col))
    spread = bf16(f32(iota((modes, size), 0) == (iota((modes, size), 1) // slots) % modes))
    wide = jnp.dot(pick, bf16(root_ref[...]), preferred_element_type=jnp.float32)
    wide = jnp.dot(bf16(wide), spread, preferred_element_type=jnp.float32)
    row, col = iota((size, size), 0), iota((size, size), 1)
    same = ((row // tall) % slots == col % slots) & ((row // levels) % taken == col // (modes * slots))
    kron[...] = bf16(jnp.where(same, wide, 0.0))
    onehot[...] = bf16(f32(iota((lat_count, lat_count), 0) == order_ref[...])).T

    def spectra(h, first, count):
        width = slots * tall
        for r in range(2):
            x = f32(ctl[h * taken : (h + 1) * taken, :, r])
            x = bf16(x.reshape(taken * modes * slots, totals))
            some = kron[first * width : (first + count) * width]
            spec = jnp.dot(some, x, preferred_element_type=jnp.float32) * loc_ref[...]
            spec = bf16(spec).reshape(count, slots, tall, totals)
            sx[first : first + count, :, r, h * tall : (h + 1) * tall] = spec

    def exchange(q, i):
        part_of = pl.ds(q * quad, quad)
        return pltpu.make_async_remote_copy(
            src_ref=sx.at[i, part_of],
            dst_ref=rx.at[i, part_of],
            send_sem=xs_sem,
            recv_sem=xr_sem.at[2 if i == 2 else q],
            device_id=(rows, turn(me, i, mem_count)),
            device_id_type=MESH,
        )

    def push(part, chunk):
        lo, n = PARTS[part]

        def send(dest):
            pltpu.make_async_remote_copy(
                src_ref=sbuf.at[chunk, dest, pl.ds(lo, n)],
                dst_ref=gbuf.at[chunk, rows, pl.ds(lo, n)],
                send_sem=as_sem,
                recv_sem=ar_sem.at[part if isinstance(chunk, int) else chunk],
                device_id=(dest, me),
                device_id_type=MESH,
            ).start()

        each_peer(send)

    def stored(s, four):
        stage[pl.ds(s, lat_count, stride=quad), :] = lax.dot_general(
            onehot[...], bf16(four), (((1,), (1,)), ((), ())), preferred_element_type=jnp.float32
        )

    def keep(chunk):
        sbuf[chunk] = bf16(stage[...]).reshape(row_count, lats * quad, LANES)
        pltpu.make_async_copy(sbuf.at[chunk, rows], gbuf.at[chunk, rows], own_sem).start()

    def legendre_packed(chunk, spec, i):
        for s in range(quad):
            four = [
                jnp.dot(
                    spec[i, q * quad + s].reshape(2 * members * levels, totals),
                    leg[q * quad + s],
                    preferred_element_type=jnp.float32,
                )
                for q in range(QUADS)
            ]
            stored(s, jnp.concatenate(four, axis=0))
        keep(chunk)

    def legendre_sides(q, carry):
        got = rx.at[1, pl.ds(0, slots)]
        pltpu.make_async_copy(got, got, xr_sem.at[q]).wait()
        for s in range(quad):
            x = jnp.concatenate(
                [rx[i, q * quad + s, r] for r in range(2) for i in (1, 3)], axis=0
            )
            stored(s, jnp.dot(x, leg[q * quad + s], preferred_element_type=jnp.float32))
        keep(SIDES + q)
        push(SIDES, SIDES + q)
        return carry

    for h in range(HALVES):
        ctl_in[h].wait()
        spectra(h, 0, 1)
    leg_in.wait()
    legendre_packed(OWN, sx, 0)
    pl.semaphore_wait(barrier, row_count + mem_count - 2)
    push(OWN, OWN)
    for h in range(HALVES):
        spectra(h, 1, mem_count - 1)
    for i in (1, 3):
        exchange(0, i).start()
    for i in (1, 3):
        exchange(1, i).start()
    for q in range(QUADS):
        exchange(q, 2).start()
    ptb_in.start()

    slot_count, lon_count = basis.shape[0] // 2, basis.shape[1]
    wave = jnp.broadcast_to(wave_ref[...], (LANES, slot_count)).T
    waves = unweave(wave.reshape(row_count, slots, LANES), quad)
    some = slot_count // QUADS
    turns = lon_count // LANES
    for q, wave in enumerate(waves):
        weight = jnp.where(wave == 0, 1.0, 2.0)
        angle = f32(lax.rem(wave * iota(wave.shape, 1), lon_count)) * (2.0 * math.pi / lon_count)
        fine_cos, fine_sin = weight * jnp.cos(angle), weight * jnp.sin(angle)
        angle = f32(lax.rem(wave * iota(wave.shape, 1), turns)) * (2.0 * math.pi / turns)
        wide_cos, wide_sin = jnp.cos(angle), jnp.sin(angle)
        for a in range(turns):
            x = pl.ds(a * LANES, LANES)
            wc = wide_cos[:, a : a + 1]
            ws = wide_sin[:, a : a + 1]
            basis[pl.ds(2 * q * some, some), x] = bf16(fine_cos * wc - fine_sin * ws)
            basis[pl.ds((2 * q + 1) * some, some), x] = bf16(-(fine_sin * wc + fine_cos * ws))
    total[...] = jnp.zeros_like(total)

    lax.fori_loop(0, QUADS, legendre_sides, 0)
    got = rx.at[2]
    pltpu.make_async_copy(got, got, xr_sem.at[2]).wait()
    legendre_packed(FAR, rx, 2)
    push(3, FAR)
    push(4, FAR)

    ptb_in.wait()
    pltpu.make_async_copy(sbuf.at[:, 0], gbuf.at[:, 0], own_sem).wait()

    def arrived(part, chunk):
        lo, n = PARTS[part]
        got = gbuf.at[chunk, pl.ds(0, row_count - 1), pl.ds(lo, n)]
        pltpu.make_async_copy(got, got, ar_sem.at[part]).wait()

    def turned(chunk, b):
        tile = pl.ds(pl.multiple_of(b * 16, 16), 16)
        got = f32(gbuf[chunk, :, tile, :])
        return [
            bf16(v).T for p in range(LATS // 2) for v in unweave(got[:, p * 8 : p * 8 + 8], quad)
        ]

    def cut(x, count):
        n = LANES // count
        return [x[c * n : (c + 1) * n] for c in range(count)]

    def zonal(b, blocks, offsets):
        lhs = jnp.concatenate([jnp.concatenate(parts, axis=1) for parts in blocks], axis=0)
        here = pl.ds(b * LATS, LATS)
        for x in range(0, lon_count, PIECE):
            field = jnp.dot(lhs, basis[:, x : x + PIECE], preferred_element_type=jnp.float32)
            field = f32(bf16(field)).reshape(LATS, len(offsets), members, levels, PIECE)
            sums = total[here, :, x : x + PIECE]
            for n, i in enumerate(offsets):
                begin = turn(me, mem_count - i, mem_count) * members
                near = f32(ptb[here, pl.ds(begin, members), :, x : x + PIECE])
                sums += jnp.sum(field[:, n] * near, axis=1)
            total[here, :, x : x + PIECE] = sums
            if offsets == (2,):
                out_ref[here, :, x : x + PIECE] = bf16(sums)

    def own_step(b, carry):
        zonal(b, [cut(t, 2 * QUADS) for t in turned(OWN, b)], (0,))
        return carry

    def sides_step(b, carry):
        pairs = zip(turned(SIDES, b), turned(SIDES + 1, b))
        zonal(b, [cut(t, 2) + cut(u, 2) for t, u in pairs], (1, 3))
        return carry

    def far_step(b, carry):
        @pl.when(b == 2)
        def _():
            arrived(4, FAR)

        zonal(b, [cut(t, 2 * QUADS) for t in turned(FAR, b)], (2,))
        return carry

    arrived(0, OWN)
    lax.fori_loop(0, lats // LATS, own_step, 0)
    arrived(1, SIDES)
    arrived(2, SIDES + 1)
    lax.fori_loop(0, lats // LATS, sides_step, 0)
    arrived(3, FAR)
    lax.fori_loop(0, lats // LATS, far_step, 0)

    sent = sx.at[pl.ds(1, mem_count - 1)]
    pltpu.make_async_copy(sent, sent, xs_sem).wait()
    sent = sbuf.at[:, pl.ds(0, row_count - 1)]
    pltpu.make_async_copy(sent, sent, as_sem).wait()


def shards(control, vert_root, loc_spec, legendre, wave_table, lat_order, perturb):
    members, modes, parts, slots, totals = control.shape
    lat_count = legendre.shape[2]
    lats, _, levels, lon_count = perturb.shape
    row_count, mem_count = 64, 4
    quad = slots // QUADS
    each = lats * quad
    size = slots * (members // HALVES) * modes
    spectra = (mem_count, slots, parts, members * levels, totals)
    small = pl.BlockSpec(memory_space=pltpu.VMEM)
    large = pl.BlockSpec(memory_space=pl.ANY)
    half = jnp.bfloat16
    return pl.pallas_call(
        kernel,
        out_shape=jax.ShapeDtypeStruct((lats, levels, lon_count), half),
        in_specs=[small, small, small, small, large, large, large],
        out_specs=small,
        scratch_shapes=[
            pltpu.VMEM(control.shape, half),
            pltpu.VMEM(legendre.shape, half),
            pltpu.VMEM(perturb.shape, half),
            pltpu.VMEM((size, size), half),
            pltpu.VMEM((lat_count, lat_count), half),
            pltpu.VMEM(spectra, half),
            pltpu.VMEM(spectra, half),
            pltpu.VMEM((lat_count * quad, LANES), jnp.float32),
            pltpu.VMEM((CHUNKS, row_count, each, LANES), half),
            pltpu.VMEM((CHUNKS, row_count, each, LANES), half),
            pltpu.VMEM((2 * row_count * slots, lon_count), half),
            pltpu.VMEM((lats, levels, lon_count), jnp.float32),
            pltpu.SemaphoreType.DMA((4,)),
            pltpu.SemaphoreType.DMA,
            pltpu.SemaphoreType.DMA((3,)),
            pltpu.SemaphoreType.DMA,
            pltpu.SemaphoreType.DMA((5,)),
            pltpu.SemaphoreType.DMA,
        ],
        compiler_params=pltpu.CompilerParams(
            collective_id=0, has_side_effects=True, vmem_limit_bytes=VMEM_LIMIT
        ),
    )(
        vert_root,
        loc_spec[None],
        lat_order[None],
        wave_table[None],
        control,
        legendre,
        perturb,
    )


def solution(mesh):
    return jax.shard_map(
        shards,
        mesh=mesh,
        in_specs=(
            P("mem", None, None, "rows", None),
            P(),
            P(),
            P("rows", None, None),
            P(),
            P(),
            P("rows", None, "mem", None),
        ),
        out_specs=P("rows", "mem", None),
        check_vma=False,
    )
```

time: 98.7 us -> 88.8 us (0.90)
  Pallas kernels: 95.6 us -> 85.7 us
    pallas_call x1, Pallas kernels: 95.6 us -> 85.7 us  [shards(): pl.pallas_call(kernel, out_shape=jax.ShapeDtypeStruct((lats, levels, lon_...]
where the time goes in v2:
time: 88.8 us; the launch traced here: 88.6 us
  Pallas kernels  85.7 us (97%)
  local copies, waits for them, and re-layouts  2.96 us (3%)
    pallas_call x1, Pallas kernels, shards(): pl.pallas_call(kernel, out_shape=jax.ShapeDtypeStruct((lats, levels, lon_...  85.7 us

profile of v2, /device:TPU:1, one launch (start us, length us, event | category | flops | bytes accessed | tf_op | source)
XLA Modules:
  0.0 88.6 jit_solution(11732618955162336787)
XLA Ops:
  0.0 1.3 %broadcast_in_dim.10.order_ref = s32[1,768]{1,0:T(1,128)} reshape(s32[768]{0:T(1024)} %param.12) | data formatting | bytes 6144 | tf_op jit(solution)/shard_map/broadcast_in_dim | solution.py:337
  1.3 85.7 %shard_map.73 = bf16[12,8,1536]{2,1,0:T(8,128)(2,1)} custom-call(f32[32,32]{1,0:T(8,128)} %root_ref.1, f32[1,512]{1,0:T(1,128)} %bitcast.2, s32[1,768]{1,0:T(1,128)} %broadcast_in_dim.10.order_ref, s32[1,512]{1,0:T(1,128)} %bitcast.3, bf16[4,32,2,8,512]{4,3,2,1,0:T(8,128)(2,1)} %ctl_hbm.1, bf16[8,512,768]{2,1,0:T(8,128)(2,1)} %leg_hbm.1, ...), custom_call_target="tpu_custom_call" | custom-call | tf_op jit(solution)/shard_map/pallas_call | solution.py:306
  86.9 1.7 %copy.9 = bf16[12,8,1536]{2,1,0:T(8,128)(2,1)} copy(bf16[12,8,1536]{2,1,0:T(8,128)(2,1)} %shard_map.73) | data formatting | bytes 589824

commit v3 on v2

--- a/solution.py
+++ b/solution.py
@@ -16,7 +16,7 @@
 OWN, SIDES, FAR = 0, 1, 3
 CHUNKS = 4
 PARTS = ((0, 48), (0, 48), (0, 48), (0, 32), (32, 16))
-VMEM_LIMIT = 60 * 1024 * 1024
+VMEM_LIMIT = 56 * 1024 * 1024
 MESH = pl.DeviceIdType.MESH
 Z, Y, CORES = 8, 4, 2
 
@@ -47,9 +47,9 @@
 
 
 def kernel(
-    root_ref, loc_ref, order_ref, wave_ref, ctl_hbm, leg_hbm, ptb_hbm, out_ref,
-    ctl, leg, ptb, kron, onehot, sx, rx, stage, sbuf, gbuf, basis, total,
-    load_sem, xs_sem, xr_sem, as_sem, ar_sem, own_sem,
+    root_hbm, loc_hbm, order_hbm, wave_hbm, ctl_hbm, leg_hbm, ptb_hbm, out_ref,
+    root_ref, loc_ref, order_ref, wave_ref, ctl, leg, ptb, kron, onehot, sx, rx, stage, sbuf, gbuf, basis, total,
+    load_sem, leg_sem, xs_sem, xr_sem, as_sem, ar_sem, own_sem,
 ):
     rows = lax.axis_index("rows")
     me = lax.axis_index("mem")
@@ -68,11 +68,19 @@
         )
         for h in range(HALVES)
     ]
-    leg_in = pltpu.make_async_copy(leg_hbm, leg, load_sem.at[2])
-    ptb_in = pltpu.make_async_copy(ptb_hbm, ptb, load_sem.at[3])
-    for c in ctl_in:
+    leg_in = [pltpu.make_async_copy(leg_hbm.at[s], leg.at[s], leg_sem.at[s]) for s in range(slots)]
+    ptb_in = pltpu.make_async_copy(ptb_hbm, ptb, load_sem.at[2])
+    root_in, loc_in, order_in, wave_in = [
+        pltpu.make_async_copy(source, kept, load_sem.at[3 + n])
+        for n, (source, kept) in enumerate(
+            ((root_hbm, root_ref), (loc_hbm, loc_ref), (order_hbm, order_ref), (wave_hbm, wave_ref))
+        )
+    ]
+    for c in (root_in, order_in, loc_in, *ctl_in, wave_in):
         c.start()
-    leg_in.start()
+
+    for s in (0, 4, 1, 5):
+        leg_in[s].start()
 
     barrier = pltpu.get_barrier_semaphore()
     z, y, core = rows // (Y * CORES), (rows // CORES) % Y, rows % CORES
@@ -100,18 +108,20 @@
         pl.semaphore_signal(
             barrier, inc=1, device_id=(rows, turn(me, i, mem_count)), device_id_type=MESH
         )
+    for s in (2, 3, 6, 7):
+        leg_in[s].start()
 
     size = slots * taken * modes
     row, col = iota((size, modes), 0), iota((size, modes), 1)
     level = lax.rem(me + row // (slots * tall), mem_count) * levels + row % levels
     pick = bf16(f32(level == col))
     spread = bf16(f32(iota((modes, size), 0) == (iota((modes, size), 1) // slots) % modes))
+    root_in.wait()
     wide = jnp.dot(pick, bf16(root_ref[...]), preferred_element_type=jnp.float32)
     wide = jnp.dot(bf16(wide), spread, preferred_element_type=jnp.float32)
     row, col = iota((size, size), 0), iota((size, size), 1)
     same = ((row // tall) % slots == col % slots) & ((row // levels) % taken == col // (modes * slots))
     kron[...] = bf16(jnp.where(same, wide, 0.0))
-    onehot[...] = bf16(f32(iota((lat_count, lat_count), 0) == order_ref[...])).T
 
     def spectra(h, first, count):
         width = slots * tall
@@ -160,14 +170,16 @@
 
     def legendre_packed(chunk, spec, i):
         for s in range(quad):
-            four = [
-                jnp.dot(
-                    spec[i, q * quad + s].reshape(2 * members * levels, totals),
-                    leg[q * quad + s],
-                    preferred_element_type=jnp.float32,
-                )
-                for q in range(QUADS)
-            ]
+            if chunk == OWN and s % 2 == 0:
+                for slot in (s, s + 1, s + quad, s + quad + 1):
+                    leg_in[slot].wait()
+            if chunk == OWN and s == 0:
+                order = order_ref[...].reshape(1, lat_count)
+                onehot[...] = bf16(f32(iota((lat_count, lat_count), 0) == order)).T
+            four = []
+            for slot in range(s, slots, quad):
+                x = spec[i, slot].reshape(2 * members * levels, totals)
+                four.append(jnp.dot(x, leg[slot], preferred_element_type=jnp.float32))
             stored(s, jnp.concatenate(four, axis=0))
         keep(chunk)
 
@@ -183,10 +195,11 @@
         push(SIDES, SIDES + q)
         return carry
 
+    order_in.wait()
+    loc_in.wait()
     for h in range(HALVES):
         ctl_in[h].wait()
         spectra(h, 0, 1)
-    leg_in.wait()
     legendre_packed(OWN, sx, 0)
     pl.semaphore_wait(barrier, row_count + mem_count - 2)
     push(OWN, OWN)
@@ -201,6 +214,7 @@
     ptb_in.start()
 
     slot_count, lon_count = basis.shape[0] // 2, basis.shape[1]
+    wave_in.wait()
     wave = jnp.broadcast_to(wave_ref[...], (LANES, slot_count)).T
     waves = unweave(wave.reshape(row_count, slots, LANES), quad)
     some = slot_count // QUADS
@@ -300,15 +314,18 @@
     each = lats * quad
     size = slots * (members // HALVES) * modes
     spectra = (mem_count, slots, parts, members * levels, totals)
-    small = pl.BlockSpec(memory_space=pltpu.VMEM)
-    large = pl.BlockSpec(memory_space=pl.ANY)
+    large = pl.BlockSpec(memory_space=pltpu.HBM)
     half = jnp.bfloat16
     return pl.pallas_call(
         kernel,
-        out_shape=jax.ShapeDtypeStruct((lats, levels, lon_count), half),
-        in_specs=[small, small, small, small, large, large, large],
-        out_specs=small,
+        out_shape=pltpu.VMEM((lats, levels, lon_count), half),
+        in_specs=[large] * 7,
+        out_specs=pl.BlockSpec(memory_space=pltpu.VMEM),
         scratch_shapes=[
+            pltpu.VMEM(vert_root.shape, jnp.float32),
+            pltpu.VMEM((1, totals), jnp.float32),
+            pltpu.VMEM(lat_order.shape, jnp.int32),
+            pltpu.VMEM((1, row_count * slots), jnp.int32),
             pltpu.VMEM(control.shape, half),
             pltpu.VMEM(legendre.shape, half),
             pltpu.VMEM(perturb.shape, half),
@@ -321,7 +338,8 @@
             pltpu.VMEM((CHUNKS, row_count, each, LANES), half),
             pltpu.VMEM((2 * row_count * slots, lon_count), half),
             pltpu.VMEM((lats, levels, lon_count), jnp.float32),
-            pltpu.SemaphoreType.DMA((4,)),
+            pltpu.SemaphoreType.DMA((7,)),
+            pltpu.SemaphoreType.DMA((slots,)),
             pltpu.SemaphoreType.DMA,
             pltpu.SemaphoreType.DMA((3,)),
             pltpu.SemaphoreType.DMA,
@@ -334,7 +352,7 @@
     )(
         vert_root,
         loc_spec[None],
-        lat_order[None],
+        lat_order,
         wave_table[None],
         control,
         legendre,

time: 88.8 us -> 84.5 us (0.952)
  local copies, waits for them, and re-layouts: 2.96 us -> 0.72 us
  Pallas kernels: 85.7 us -> 83.6 us
    pallas_call x1, Pallas kernels: 85.7 us -> 83.6 us  [shards(): pl.pallas_call(kernel, out_shape=pltpu.VMEM((lats, levels, lon_count), ha...]
    broadcast_in_dim x1 -> x0, local copies, waits for them, and re-layouts: 1.27 us -> none  [shards(): lat_order[None]]
    unnamed x1, local copies, waits for them, and re-layouts: 1.69 us -> 0.72 us
where the time goes in v3:
time: 84.5 us; the launch traced here: 84.4 us
  Pallas kernels  83.6 us (99%)
    pallas_call x1, Pallas kernels, shards(): pl.pallas_call(kernel, out_shape=pltpu.VMEM((lats, levels, lon_count), ha...  83.6 us

profile of v3, /device:TPU:1, one launch (start us, length us, event | category | flops | bytes accessed | tf_op | source)
XLA Modules:
  0.0 84.4 jit_solution(17584022309581732923)
XLA Ops:
  0.0 83.6 %shard_map.73 = bf16[12,8,1536]{2,1,0:T(8,128)(2,1)S(1)} custom-call(f32[32,32]{1,0:T(8,128)} %root_hbm.1, f32[1,512]{1,0:T(1,128)} %bitcast.2, s32[768]{0:T(1024)} %order_hbm.1, s32[1,512]{1,0:T(1,128)} %bitcast.3, bf16[4,32,2,8,512]{4,3,2,1,0:T(8,128)(2,1)} %ctl_hbm.1, bf16[8,512,768]{2,1,0:T(8,128)(2,1)} %leg_hbm.1, bf16[12,16,8,1536]{3,2,1,0:T(8,128)(2,1)} %ptb_hbm.1), custom_call_target="tpu_custom_call" | custom-call | tf_op jit(solution)/shard_map/pallas_call | solution.py:319
  83.6 0.7 copy.9

commit v4 on v3

--- a/solution.py
+++ b/solution.py
@@ -152,47 +152,55 @@
                 src_ref=sbuf.at[chunk, dest, pl.ds(lo, n)],
                 dst_ref=gbuf.at[chunk, rows, pl.ds(lo, n)],
                 send_sem=as_sem,
-                recv_sem=ar_sem.at[part if isinstance(chunk, int) else chunk],
+                recv_sem=ar_sem.at[part],
                 device_id=(dest, me),
                 device_id_type=MESH,
             ).start()
 
         each_peer(send)
 
-    def stored(s, four):
-        stage[pl.ds(s, lat_count, stride=quad), :] = lax.dot_general(
-            onehot[...], bf16(four), (((1,), (1,)), ((), ())), preferred_element_type=jnp.float32
-        )
+    def stored(s, fours):
+        rows_of = lax.dot_general(
+            onehot[...],
+            jnp.concatenate([bf16(f) for f in fours], axis=0),
+            (((1,), (1,)), ((), ())),
+            preferred_element_type=jnp.float32,
+        )
+        for n in range(2):
+            stage[pl.ds(s + n, lat_count, stride=quad), :] = rows_of[:, n * LANES : (n + 1) * LANES]
 
     def keep(chunk):
         sbuf[chunk] = bf16(stage[...]).reshape(row_count, lats * quad, LANES)
         pltpu.make_async_copy(sbuf.at[chunk, rows], gbuf.at[chunk, rows], own_sem).start()
 
     def legendre_packed(chunk, spec, i):
-        for s in range(quad):
-            if chunk == OWN and s % 2 == 0:
+        fours = []
+        for s in range(0, quad, 2):
+            if chunk == OWN:
                 for slot in (s, s + 1, s + quad, s + quad + 1):
                     leg_in[slot].wait()
             if chunk == OWN and s == 0:
                 order = order_ref[...].reshape(1, lat_count)
                 onehot[...] = bf16(f32(iota((lat_count, lat_count), 0) == order)).T
             four = []
-            for slot in range(s, slots, quad):
+            for slot in (s, s + quad, s + 1, s + quad + 1):
                 x = spec[i, slot].reshape(2 * members * levels, totals)
-                four.append(jnp.dot(x, leg[slot], preferred_element_type=jnp.float32))
-            stored(s, jnp.concatenate(four, axis=0))
+                four.append(bf16(jnp.dot(x, leg[slot], preferred_element_type=jnp.float32)))
+            fours.append(four)
+        for n, four in enumerate(fours):
+            stored(2 * n, four)
         keep(chunk)
 
     def legendre_sides(q, carry):
         got = rx.at[1, pl.ds(0, slots)]
         pltpu.make_async_copy(got, got, xr_sem.at[q]).wait()
-        for s in range(quad):
-            x = jnp.concatenate(
-                [rx[i, q * quad + s, r] for r in range(2) for i in (1, 3)], axis=0
-            )
-            stored(s, jnp.dot(x, leg[q * quad + s], preferred_element_type=jnp.float32))
+        for s in range(0, quad, 2):
+            four = []
+            for slot in (q * quad + s, q * quad + s + 1):
+                x = jnp.concatenate([rx[i, slot, r] for r in range(2) for i in (1, 3)], axis=0)
+                four.append(jnp.dot(x, leg[slot], preferred_element_type=jnp.float32))
+            stored(s, four)
         keep(SIDES + q)
-        push(SIDES, SIDES + q)
         return carry
 
     order_in.wait()
@@ -234,6 +242,7 @@
     total[...] = jnp.zeros_like(total)
 
     lax.fori_loop(0, QUADS, legendre_sides, 0)
+    push(1, pl.ds(SIDES, QUADS))
     got = rx.at[2]
     pltpu.make_async_copy(got, got, xr_sem.at[2]).wait()
     legendre_packed(FAR, rx, 2)
@@ -293,8 +302,7 @@
 
     arrived(0, OWN)
     lax.fori_loop(0, lats // LATS, own_step, 0)
-    arrived(1, SIDES)
-    arrived(2, SIDES + 1)
+    arrived(1, pl.ds(SIDES, QUADS))
     lax.fori_loop(0, lats // LATS, sides_step, 0)
     arrived(3, FAR)
     lax.fori_loop(0, lats // LATS, far_step, 0)

time: 84.5 us -> 84.3 us (level)
  no operation moved by 1% of the time
where the time goes in v4:
time: 84.3 us; the launch traced here: 84.1 us
  Pallas kernels  83.4 us (99%)
    pallas_call x1, Pallas kernels, shards(): pl.pallas_call(kernel, out_shape=pltpu.VMEM((lats, levels, lon_count), ha...  83.4 us

profile of v4, /device:TPU:1, one launch (start us, length us, event | category | flops | bytes accessed | tf_op | source)
XLA Modules:
  0.0 84.1 jit_solution(7784938143237028643)
XLA Ops:
  0.0 83.4 %shard_map.73 = bf16[12,8,1536]{2,1,0:T(8,128)(2,1)S(1)} custom-call(f32[32,32]{1,0:T(8,128)} %root_hbm.1, f32[1,512]{1,0:T(1,128)} %bitcast.2, s32[768]{0:T(1024)} %order_hbm.1, s32[1,512]{1,0:T(1,128)} %bitcast.3, bf16[4,32,2,8,512]{4,3,2,1,0:T(8,128)(2,1)} %ctl_hbm.1, bf16[8,512,768]{2,1,0:T(8,128)(2,1)} %leg_hbm.1, bf16[12,16,8,1536]{3,2,1,0:T(8,128)(2,1)} %ptb_hbm.1), custom_call_target="tpu_custom_call" | custom-call | tf_op jit(solution)/shard_map/pallas_call | solution.py:327
  83.4 0.7 copy.9

commit v5 on v4

--- a/solution.py
+++ b/solution.py
@@ -85,7 +85,7 @@
     barrier = pltpu.get_barrier_semaphore()
     z, y, core = rows // (Y * CORES), (rows // CORES) % Y, rows % CORES
     spots = [
-        turn(y, w // CORES + 1, Y) * CORES + turn(core, w + 1, CORES) for w in range(Y * CORES)
+        turn(y, dy, Y) * CORES + turn(core, dc, CORES) for dy in (2, 1, 3, 0) for dc in (1, 0)
     ]
 
     def each_peer(act):

time: 84.3 us -> 84.3 us (level)
  no operation moved by 1% of the time
where the time goes in v5:
time: 84.3 us; the launch traced here: 84.2 us
  Pallas kernels  83.5 us (99%)
    pallas_call x1, Pallas kernels, shards(): pl.pallas_call(kernel, out_shape=pltpu.VMEM((lats, levels, lon_count), ha...  83.5 us

profile of v5, /device:TPU:1, one launch (start us, length us, event | category | flops | bytes accessed | tf_op | source)
XLA Modules:
  0.0 84.2 jit_solution(11935314207553862343)
XLA Ops:
  0.0 83.5 %shard_map.73 = bf16[12,8,1536]{2,1,0:T(8,128)(2,1)S(1)} custom-call(f32[32,32]{1,0:T(8,128)} %root_hbm.1, f32[1,512]{1,0:T(1,128)} %bitcast.2, s32[768]{0:T(1024)} %order_hbm.1, s32[1,512]{1,0:T(1,128)} %bitcast.3, bf16[4,32,2,8,512]{4,3,2,1,0:T(8,128)(2,1)} %ctl_hbm.1, bf16[8,512,768]{2,1,0:T(8,128)(2,1)} %leg_hbm.1, bf16[12,16,8,1536]{3,2,1,0:T(8,128)(2,1)} %ptb_hbm.1), custom_call_target="tpu_custom_call" | custom-call | tf_op jit(solution)/shard_map/pallas_call | solution.py:327
  83.5 0.7 copy.9
